TPU v7x, 32 devices: a whole 2x2x4 slice. The times are simulated.
32 devices in a mesh: seq: 4 (over y, core), blk: 8 (over z, x).
Axes of the slice: x: 2, y: 2, z: 4, core: 2. Of those that a mesh axis runs over, the one named last changes fastest.
Arguments:
- kv_cache: bfloat16 [4, 2, 16, 4096, 1024], P(None, None, None, ('seq', 'blk')), may hold values from -18 to 18, as said below
- queries: bfloat16 [4, 128, 1024], P(None, 'blk'), may hold values from -400 to 400
- fresh_key_value: bfloat16 [4, 2, 128, 128], P(None, None, 'blk'), may hold values from -70 to 70
- lengths: int32 [16], replicated, may hold values from 1 to 4096, 49152 in all
Outputs:
- quant_cache: bfloat16 [4, 2, 128, 4096, 128], P(None, None, 'blk', 'seq')
- block_scale: float32 [4, 2, 128, 32], P(None, None, 'blk', 'seq')
- attended: bfloat16 [4, 128, 1024], P(None, 'blk')
Inputs may be any that keep to these rules, and one draw needn't show every extreme that they name: `kv_cache`: each entry is a random value times a factor drawn for its position and head. `lengths`: every sequence has at least one live position, and some sequence uses all 4096.
All inputs are finite; a program needn't handle non-finite values.
Results may differ from a plain program's by a relative error of at most 0.003.
The roundings to bfloat16 on the way count: a program that leaves them out, or rounds other values in their place, can miss the bound.
Values may be sent and summed in bfloat16 or wider, within the bound.
No kernel may reach another device: no remote copies, remote signals or barrier semaphores. Data moves between devices by JAX's collectives and lax.ppermute only.
A program may use at most 192 MiB of HBM per device.

v0:
```python
import jax
import jax.numpy as jnp
from jax import lax
from jax.sharding import PartitionSpec as P

HEAD_DIM = 128
QUERY_GROUP = 8
BLOCK = 128


def on_device(kv_cache, queries, fresh_key_value, lengths):
    layers, _, batch, local_rows, width = kv_cache.shape
    heads = width // HEAD_DIM
    blk_count = lax.axis_size("blk")
    blk_place = lax.axis_index("blk")
    pairs_here = heads * batch // blk_count
    seq_rows = local_rows * blk_count
    blocks_here = seq_rows // BLOCK
    arranged = kv_cache.reshape(layers, 2, batch, local_rows, heads, HEAD_DIM).transpose(
        0, 1, 4, 2, 3, 5
    )
    arranged = arranged.reshape(layers, 2, heads * batch, local_rows, HEAD_DIM)
    pair_start = blk_place * pairs_here
    moved = lax.all_to_all(arranged, "blk", split_axis=2, concat_axis=3, tiled=True)
    grouped = moved.reshape(layers, 2, pairs_here, blocks_here, BLOCK, HEAD_DIM)
    block_scale = (
        jnp.maximum(jnp.max(jnp.abs(grouped), axis=(4, 5)).astype(jnp.float32), 1.0) / 127.0
    )
    quant = (grouped.astype(jnp.float32) / block_scale[..., None, None]).astype(jnp.bfloat16)
    quant = quant.reshape(layers, 2, pairs_here, seq_rows, HEAD_DIM)
    seq_start = lax.axis_index("seq") * seq_rows
    pair_len = lax.dynamic_slice_in_dim(jnp.tile(lengths, heads), pair_start, pairs_here)
    positions = seq_start + jnp.arange(seq_rows, dtype=jnp.int32).reshape(blocks_here, BLOCK)
    valid = positions[None] < pair_len[:, None, None]
    inverse = 1.0 / jnp.sqrt(jnp.float32(HEAD_DIM))
    grouped_queries = queries.reshape(layers, pairs_here, QUERY_GROUP, HEAD_DIM)
    peaks = []
    totals = []
    sums = []
    for layer in range(layers):
        raw = jnp.einsum(
            "pgd,prd->pgr",
            grouped_queries[layer],
            quant[layer, 0],
            preferred_element_type=jnp.float32,
        )
        scores = (
            raw.reshape(pairs_here, QUERY_GROUP, blocks_here, BLOCK)
            * block_scale[layer, 0][:, None, :, None]
            * inverse
        )
        masked = jnp.where(valid[:, None], scores, -1e30)
        block_top = jnp.max(masked, axis=-1)
        weight = jnp.where(valid[:, None], jnp.exp(masked - block_top[..., None]), 0.0)
        block_total = jnp.sum(weight, axis=-1)
        rounded = (weight * block_scale[layer, 1][:, None, :, None]).astype(jnp.bfloat16)
        values = quant[layer, 1].reshape(pairs_here, blocks_here, BLOCK, HEAD_DIM)
        block_sum = jnp.einsum(
            "pgnt,pntd->pgnd", rounded, values, preferred_element_type=jnp.float32
        )
        local_top = jnp.max(block_top, axis=-1)
        scale_factor = jnp.exp(block_top - local_top[..., None])
        peaks.append(local_top)
        totals.append(jnp.sum(scale_factor * block_total, axis=-1))
        sums.append(jnp.sum(scale_factor[..., None] * block_sum, axis=2))
    peak = jnp.stack(peaks)
    total = jnp.stack(totals)
    weighted = jnp.stack(sums)
    shared_top = lax.pmax(peak, "seq")
    scale_factor = jnp.exp(peak - shared_top)
    total, weighted = lax.psum((total * scale_factor, weighted * scale_factor[..., None]), "seq")
    peak = shared_top
    own = (
        jnp.einsum(
            "lpgd,lpd->lpg",
            grouped_queries,
            fresh_key_value[:, 0],
            preferred_element_type=jnp.float32,
        )
        * inverse
    )
    top = jnp.maximum(peak, own)
    cache_w = jnp.exp(peak - top)
    own_w = jnp.exp(own - top)
    numer = (
        weighted * cache_w[..., None]
        + own_w[..., None] * fresh_key_value[:, 1].astype(jnp.float32)[:, :, None, :]
    )
    denom = total * cache_w + own_w
    attended = (
        (numer / denom[..., None])
        .reshape(layers, pairs_here, QUERY_GROUP * HEAD_DIM)
        .astype(jnp.bfloat16)
    )
    return (quant, block_scale, attended)


def solution(mesh):
    in_specs = (
        P(None, None, None, ("seq", "blk"), None),
        P(None, "blk", None),
        P(None, None, "blk", None),
        P(),
    )
    out_specs = (
        P(None, None, "blk", "seq", None),
        P(None, None, "blk", "seq"),
        P(None, "blk", None),
    )
    return jax.shard_map(
        on_device, mesh=mesh, in_specs=in_specs, out_specs=out_specs, check_vma=False
    )
```

profile of v0, /device:TPU:0, one launch (start us, length us, event | category | flops | bytes accessed | tf_op | source)
XLA Modules:
  0.0 1028.5 jit_solution(197977357570739834)
XLA Ops:
  7.2 43.9 %copy.101 = bf16[4,2,16,128,1024]{3,4,2,1,0:T(8,128)(2,1)} copy(bf16[4,2,16,128,1024]{4,3,2,1,0:T(8,128)(2,1)} %param.4) | data formatting | bytes 67108864 | tf_op args[0]
  51.0 42.3 %copy.102 = bf16[4,2,8,16,128,128]{5,4,3,2,1,0:T(8,128)(2,1)} copy(bf16[4,2,8,16,128,128]{4,5,2,3,1,0:T(8,128)(2,1)} %bitcast.243) | data formatting | bytes 67108864 | tf_op jit(solution)/shard_map/transpose | solution.py:19
  93.4 22.9 %copy.103 = bf16[4,2,128,128,128]{4,3,1,0,2:T(8,128)(2,1)} copy(bf16[4,2,128,128,128]{4,3,2,1,0:T(8,128)(2,1)} %bitcast.241) | data formatting | bytes 67108864 | tf_op jit(solution)/shard_map/reshape | solution.py:22
  116.3 7.4 all-to-all-start
  124.6 723.3 %all-to-all-done = bf16[4,2,128,128,128]{4,3,1,0,2:T(8,128)(2,1)} async-done(((bf16[4,2,128,128,128]{4,3,1,0,2:T(8,128)(2,1)}), bf16[4,2,128,128,128]{4,3,1,0,2:T(8,128)(2,1)}, u32[]{:S(2)}, u32[]{:S(2)}) %all-to-all-start) | async-done | bytes 33554464 | tf_op jit(solution)/shard_map/all_to_all | solution.py:24
  847.9 11.5 %abs_reduce_fusion = bf16[4,2,128]{1,0,2:T(4,128)(2,1)S(1)} fusion(bf16[4,2,128,128,128]{4,3,1,0,2:T(8,128)(2,1)} %all-to-all-done), kind=kLoop, calls=%fused_computation.3 | loop fusion | flops 33553408 | bytes 33556480 | tf_op jit(solution)/shard_map/reduce_max | solution.py:27
  859.8 23.0 %copy.104 = bf16[4,2,128,128,128]{4,3,2,1,0:T(8,128)(2,1)} copy(bf16[4,2,128,128,128]{4,3,1,0,2:T(8,128)(2,1)} %all-to-all-done) | data formatting | bytes 67108864 | tf_op jit(solution)/shard_map/all_to_all | solution.py:24
  882.8 23.3 %fusion.1 = bf16[4,2,16,8,128,128]{5,4,2,3,1,0:T(8,128)(2,1)} fusion(bf16[4,2,8,16,128,128]{5,4,3,2,1,0:T(8,128)(2,1)} %bitcast.242, f32[4,2,16,8]{2,3,1,0:T(8,128)S(1)} %bitcast.258), kind=kLoop, calls=%fused_computation.2 | loop fusion | flops 50331648 | bytes 67112960 | tf_op jit(solution)/shard_map/convert_element_type | solution.py:29
  906.1 22.9 %copy.106 = bf16[4,2,16,8,128,128]{5,4,3,2,1,0:T(8,128)(2,1)} copy(bf16[4,2,16,8,128,128]{5,4,2,3,1,0:T(8,128)(2,1)} %fusion.1) | data formatting | bytes 67108864 | tf_op jit(solution)/shard_map/convert_element_type | solution.py:29
  929.0 12.2 %fusion.90 = (bf16[1,1,16,1024,128]{4,3,2,1,0:T(8,128)(2,1)}, bf16[1,1,16,1024,128]{4,3,2,1,0:T(8,128)(2,1)}, bf16[1,1,16,1024,128]{4,3,2,1,0:T(8,128)(2,1)}, bf16[1,1,16,1024,128]{4,3,2,1,0:T(8,128)(2,1)}) fusion(bf16[4,2,16,1024,128]{4,3,2,1,0:T(8,128)(2,1)} %bitcast.244), kind=kLoop, calls=%fused_computation.153 | loop fusion | bytes 33554432 | tf_op jit(solution)/shard_map/slice | solution.py:57
  941.2 3.4 fusion.2
  944.5 3.4 fusion.3
  948.5 3.5 fusion.38
  952.0 3.1 fusion.34
  956.0 10.1 pmax.7
  966.1 1.5 fusion.35
  968.0 10.3 %psum.15 = f32[4,16,8]{1,2,0:T(8,128)S(1)} all-reduce(f32[4,16,8]{1,2,0:T(8,128)S(1)} %get-tuple-element.17), channel_id=1, replica_groups=mesh['seq'=4,'blk'=8] {'seq'}, use_global_device_ids=true, to_apply=%region_23.24 | all-reduce | flops 512 | bytes 4096 | tf_op jit(solution)/shard_map/psum | solution.py:71
  978.7 3.6 fusion.13
  982.3 1.3 fusion.12
  983.6 0.9 copy-done.1
  984.5 1.3 fusion.11
  986.0 1.3 fusion.10
  988.5 31.2 %all-reduce.2.cloned.1.call-done = f32[4,16,8,128]{3,2,1,0:T(8,128)} async-done(((f32[4,16,8,128]{3,2,1,0:T(8,128)}), f32[4,16,8,128]{3,2,1,0:T(8,128)}) %all-reduce.2.cloned.1.call-update) | async-done | bytes 262160 | tf_op jit(solution)/shard_map/psum | solution.py:71
  1019.7 1.2 divide_convert_fusion
  (70 shorter events, 5.5 us)
Async XLA Ops:
  116.3 7.5 copy-start.6
  116.3 7.6 copy-start.3
  116.3 7.7 copy-start.5
  116.3 731.5 %all-to-all-start = ((bf16[4,2,128,128,128]{4,3,1,0,2:T(8,128)(2,1)}), bf16[4,2,128,128,128]{4,3,1,0,2:T(8,128)(2,1)}, u32[]{:S(2)}, u32[]{:S(2)}) async-start(bf16[4,2,128,128,128]{4,3,1,0,2:T(8,128)(2,1)} %copy.103), calls=%async_computation | async-start | bytes 67108864 | tf_op jit(solution)/shard_map/all_to_all | solution.py:24
  123.7 896.0 %all-reduce.2.cloned.1.call-start = ((), (), s32[]{:S(2)}) async-start(), calls=%async_computation.1 | async-start | bytes 524288 | tf_op jit(solution)/shard_map/psum | solution.py:71
  859.7 23.1 %copy-start.4 = (f32[4,2,8,16]{3,2,1,0:T(8,128)}, f32[4,2,8,16]{3,2,1,0:T(8,128)S(1)}, u32[]{:S(2)}) copy-start(f32[4,2,8,16]{3,2,1,0:T(8,128)S(1)} %copy.105) | copy-start | bytes 12292
  978.7 3.6 copy-start.2
  982.3 2.2 copy-start.1
  983.6 2.4 copy-start
Sparse Core Ops, SparseCore 0:
  988.3 31.3 all-reduce.1
where the time goes:
time: 1030 us
  waiting for transfers between devices  755 us (73%)
  local copies, waits for them, and re-layouts  171 us (17%)
  other arithmetic  39.3 us (4%)
  matrix products  21.1 us (2%)
  blocking collectives  20.4 us (2%)
  between operations  14.3 us (1%)
    all_to_all x1, waiting for transfers between devices, on_device(): lax.all_to_all(arranged, 'blk', split_axis=2, concat_axis=3, tiled=True)  723 us
    unnamed x25, local copies, waits for them, and re-layouts  45.2 us
    transpose x1, local copies, waits for them, and re-layouts, on_device(): kv_cache.reshape(layers, 2, batch, local_rows, heads, HEAD_DIM)  42.3 us
    psum x1, waiting for transfers between devices, on_device(): lax.psum((total * scale_factor, weighted * scale_factor[..., None]), 'seq')  31.2 us
    convert_element_type x1, other arithmetic, on_device(): (grouped.astype(jnp.float32) / block_scale[..., None, None]).astype(jnp.b...  23.3 us
    all_to_all x1, local copies, waits for them, and re-layouts, on_device(): lax.all_to_all(arranged, 'blk', split_axis=2, concat_axis=3, tiled=True)  23 us
    reshape x1, local copies, waits for them, and re-layouts, on_device(): arranged = arranged.reshape(layers, 2, heads * batch, local_rows, HEAD_DIM)  22.9 us
    convert_element_type x1, local copies, waits for them, and re-layouts, on_device(): (grouped.astype(jnp.float32) / block_scale[..., None, None]).astype(jnp.b...  22.9 us
  transfers between devices with their start and end apart: 2, of which 2 were waited for; matrix products, arithmetic and copies ran while one was open for 0% of the time, Pallas kernels for 0%

commit v1 on v0

--- a/solution.py
+++ b/solution.py
@@ -21,7 +21,10 @@
     )
     arranged = arranged.reshape(layers, 2, heads * batch, local_rows, HEAD_DIM)
     pair_start = blk_place * pairs_here
-    moved = lax.all_to_all(arranged, "blk", split_axis=2, concat_axis=3, tiled=True)
+    moved = jnp.concatenate(
+        lax.all_to_all(jnp.stack(jnp.split(arranged, lax.axis_size("blk"), axis=2)), "blk", 0, 0),
+        axis=3,
+    )
     grouped = moved.reshape(layers, 2, pairs_here, blocks_here, BLOCK, HEAD_DIM)
     block_scale = (
         jnp.maximum(jnp.max(jnp.abs(grouped), axis=(4, 5)).astype(jnp.float32), 1.0) / 127.0

time: 1030 us -> 964 us (0.936)
  local copies, waits for them, and re-layouts: 171 us -> 99.5 us
    transpose x1 -> x0, local copies, waits for them, and re-layouts: 42.3 us -> none  [on_device(): kv_cache.reshape(layers, 2, batch, local_rows, heads, HEAD_DIM)]
    all_to_all x1 -> x0, local copies, waits for them, and re-layouts: 23 us -> none  [on_device(): lax.all_to_all(arranged, 'blk', split_axis=2, concat_axis=3, tiled=True)]
    unnamed x25, local copies, waits for them, and re-layouts: 45.2 us -> 34.1 us
where the time goes in v1:
time: 964 us; the launch traced here: 963 us
  waiting for transfers between devices  755 us (78%)
  local copies, waits for them, and re-layouts  99.5 us (10%)
  other arithmetic  39.1 us (4%)
  matrix products  27.4 us (3%)
  blocking collectives  20.4 us (2%)
  between operations  14.3 us (1%)
    all_to_all x1, waiting for transfers between devices, on_device(): lax.all_to_all(jnp.stack(jnp.split(arranged, lax.axis_size('blk'), axis=2...  723 us
    unnamed x25, local copies, waits for them, and re-layouts  34.1 us
    psum x1, waiting for transfers between devices, on_device(): lax.psum((total * scale_factor, weighted * scale_factor[..., None]), 'seq')  31.2 us
    reshape x1, local copies, waits for them, and re-layouts, on_device(): kv_cache.reshape(layers, 2, batch, local_rows, heads, HEAD_DIM)  23.5 us
    convert_element_type x1, other arithmetic, on_device(): (grouped.astype(jnp.float32) / block_scale[..., None, None]).astype(jnp.b...  23.2 us
    convert_element_type x1, local copies, waits for them, and re-layouts, on_device(): (grouped.astype(jnp.float32) / block_scale[..., None, None]).astype(jnp.b...  22.9 us
  transfers between devices with their start and end apart: 2, of which 2 were waited for; matrix products, arithmetic and copies ran while one was open for 0% of the time, Pallas kernels for 0%

profile of v1, /device:TPU:0, one launch (start us, length us, event | category | flops | bytes accessed | tf_op | source)
XLA Modules:
  0.0 962.7 jit_solution(13366596551903494064)
XLA Ops:
  7.2 23.5 %copy_bitcast_fusion = bf16[4,2,16,128,8,128]{5,3,2,4,1,0:T(8,128)(2,1)} fusion(bf16[4,2,16,128,1024]{4,3,2,1,0:T(8,128)(2,1)} %param.4), kind=kLoop, calls=%fused_computation.2 | loop fusion | bytes 67108864 | tf_op jit(solution)/shard_map/reshape | solution.py:19
  30.6 4.8 fusion.12
  35.5 4.7 fusion.11
  40.2 4.7 fusion.10
  44.9 4.7 fusion.9
  49.6 4.8 fusion.8
  54.4 4.7 fusion.7
  59.1 4.7 fusion.6
  63.8 4.7 fusion.5
  68.5 7.4 all-to-all-start
  76.8 723.3 %all-to-all-done = bf16[8,4,2,16,128,128]{5,4,3,2,1,0:T(8,128)(2,1)} async-done(((bf16[8,4,2,16,128,128]{5,4,3,2,1,0:T(8,128)(2,1)}), bf16[8,4,2,16,128,128]{5,4,3,2,1,0:T(8,128)(2,1)}, u32[]{:S(2)}, u32[]{:S(2)}) %all-to-all-start) | async-done | bytes 33554464 | tf_op jit(solution)/shard_map/all_to_all | solution.py:25
  800.0 11.4 %abs_reduce_fusion = bf16[8,4,2,16]{3,2,1,0:T(2,128)(2,1)S(1)} fusion(bf16[8,4,2,16,128,128]{5,4,3,2,1,0:T(8,128)(2,1)} %all-to-all-done), kind=kLoop, calls=%fused_computation.3 | loop fusion | flops 33553408 | bytes 33556480 | tf_op jit(solution)/shard_map/reduce_max | solution.py:30
  812.4 23.2 %fusion = bf16[4,2,16,8,128,128]{5,4,2,1,0,3:T(8,128)(2,1)} fusion(bf16[8,4,2,16,128,128]{5,4,3,2,1,0:T(8,128)(2,1)} %all-to-all-done, f32[4,2,16,8]{2,1,0,3:T(2,128)S(1)} %copy.38), kind=kLoop, calls=%fused_computation.1 | loop fusion | flops 50331648 | bytes 67112960 | tf_op jit(solution)/shard_map/convert_element_type | solution.py:32
  835.6 22.9 %copy.39 = bf16[4,2,16,8,128,128]{5,4,3,2,1,0:T(8,128)(2,1)} copy(bf16[4,2,16,8,128,128]{5,4,2,1,0,3:T(8,128)(2,1)} %fusion) | data formatting | bytes 67108864 | tf_op jit(solution)/shard_map/convert_element_type | solution.py:32
  858.5 12.2 %fusion.97 = (bf16[1,1,16,1024,128]{4,3,2,1,0:T(8,128)(2,1)}, bf16[1,1,16,1024,128]{4,3,2,1,0:T(8,128)(2,1)}, bf16[1,1,16,1024,128]{4,3,2,1,0:T(8,128)(2,1)}, bf16[1,1,16,1024,128]{4,3,2,1,0:T(8,128)(2,1)}) fusion(bf16[4,2,16,1024,128]{4,3,2,1,0:T(8,128)(2,1)} %bitcast.289), kind=kLoop, calls=%fused_computation.169 | loop fusion | bytes 33554432 | tf_op jit(solution)/shard_map/slice | solution.py:60
  874.0 3.4 fusion.2
  877.8 3.5 fusion.45
  885.3 10.1 %pmax.7 = f32[4,16,8]{1,2,0:T(8,128)S(1)} all-reduce(f32[4,16,8]{1,2,0:T(8,128)S(1)} %pad_maximum_fusion), channel_id=1, replica_groups=mesh['seq'=4,'blk'=8] {'seq'}, use_global_device_ids=true, to_apply=%region_13.14 | all-reduce | flops 512 | bytes 4096 | tf_op jit(solution)/shard_map/pmax | solution.py:72
  897.3 10.3 %psum.15 = f32[4,16,8]{1,2,0:T(8,128)S(1)} all-reduce(f32[4,16,8]{1,2,0:T(8,128)S(1)} %get-tuple-element.20), channel_id=1, replica_groups=mesh['seq'=4,'blk'=8] {'seq'}, use_global_device_ids=true, to_apply=%region_23.24 | all-reduce | flops 512 | bytes 4096 | tf_op jit(solution)/shard_map/psum | solution.py:74
  907.7 3.5 fusion.20
  911.2 3.5 fusion.19
  914.6 3.5 fusion.18
  918.1 3.5 fusion.17
  922.7 31.2 %all-reduce.2.cloned.1.call-done = f32[4,16,8,128]{3,2,1,0:T(8,128)} async-done(((f32[4,16,8,128]{3,2,1,0:T(8,128)}), f32[4,16,8,128]{3,2,1,0:T(8,128)}) %all-reduce.2.cloned.1.call-update) | async-done | bytes 262160 | tf_op jit(solution)/shard_map/psum | solution.py:74
  (61 shorter events, 14.4 us)
Async XLA Ops:
  68.5 7.5 copy-start.2
  68.5 7.6 copy-start
  68.5 7.7 copy-start.1
  68.5 731.5 %all-to-all-start = ((bf16[8,4,2,16,128,128]{5,4,3,2,1,0:T(8,128)(2,1)}), bf16[8,4,2,16,128,128]{5,4,3,2,1,0:T(8,128)(2,1)}, u32[]{:S(2)}, u32[]{:S(2)}) async-start(bf16[8,4,2,16,128,128]{5,4,3,2,1,0:T(8,128)(2,1)} %fusion.5), calls=%async_computation | async-start | bytes 67108864 | tf_op jit(solution)/shard_map/all_to_all | solution.py:25
  75.9 878.0 %all-reduce.2.cloned.1.call-start = ((), (), s32[]{:S(2)}) async-start(), calls=%async_computation.1 | async-start | bytes 524288 | tf_op jit(solution)/shard_map/psum | solution.py:74
Sparse Core Ops, SparseCore 0:
  922.6 31.3 all-reduce.1
